TPU v7x, 8 devices: a whole 2x2x1 slice. The times are simulated.
8 devices in a mesh: rep: 1 (over z), head: 2 (over y), seq: 4 (over x, core).
Axes of the slice: x: 2, y: 2, z: 1, core: 2. Of those that a mesh axis runs over, the one named last changes fastest.
Arguments:
- tokens: bfloat16 [32, 3072], P('rep')
- w_query: bfloat16 [3072, 4096], replicated
- w_key: bfloat16 [3072, 4096], replicated
- w_value: bfloat16 [3072, 4096], replicated
- w_out: bfloat16 [4096, 3072], P(('head', 'seq'))
- k_cache: bfloat16 [32, 1024, 16, 256], P('rep', 'seq', 'head')
- v_cache: bfloat16 [32, 1024, 16, 256], P('rep', 'seq', 'head')
- positions: int32 [32], P('rep')
Outputs:
- output 1: bfloat16 [32, 3072], P('rep')
- output 2: bfloat16 [32, 1024, 16, 256], P('rep', 'seq', 'head')
- output 3: bfloat16 [32, 1024, 16, 256], P('rep', 'seq', 'head')
All inputs are finite; a program needn't handle non-finite values.
Results may differ from a plain program's by a relative error of at most 0.00595572.
Values are sent between devices in bfloat16 or wider.
A program may use at most 1 GiB of HBM per device.

v0:
```python
import jax
import jax.numpy as jnp
from jax import lax
from jax.sharding import PartitionSpec as P


def solution(mesh):
    head_devs = mesh.shape['head']
    cache_spec = P('rep', 'seq', 'head', None)

    def local_step(tokens, w_query, w_key, w_value, w_out, k_cache, v_cache, positions):
        batch_size, shard_len, kv_local, head_dim = k_cache.shape
        heads_total = w_query.shape[1] // head_dim
        groups = heads_total // (kv_local * head_devs)
        q_cols = kv_local * groups * head_dim
        kv_cols = kv_local * head_dim
        wo_rows = w_out.shape[0]
        head_idx = lax.axis_index('head')
        seq_idx = lax.axis_index('seq')
        wq_local = lax.dynamic_slice_in_dim(w_query, head_idx * q_cols, q_cols, axis=1)
        wk_local = lax.dynamic_slice_in_dim(w_key, head_idx * kv_cols, kv_cols, axis=1)
        wv_local = lax.dynamic_slice_in_dim(w_value, head_idx * kv_cols, kv_cols, axis=1)
        query = jnp.dot(tokens, wq_local, preferred_element_type=jnp.float32).astype(jnp.bfloat16).reshape(batch_size, kv_local, groups, head_dim)
        new_key = jnp.dot(tokens, wk_local, preferred_element_type=jnp.float32).astype(jnp.bfloat16).reshape(batch_size, 1, kv_local, head_dim)
        new_value = jnp.dot(tokens, wv_local, preferred_element_type=jnp.float32).astype(jnp.bfloat16).reshape(batch_size, 1, kv_local, head_dim)
        slot_ids = seq_idx * shard_len + jnp.arange(shard_len, dtype=jnp.int32)
        is_slot = (slot_ids[None, :] == positions[:, None])[:, :, None, None]
        k_new = jnp.where(is_slot, new_key, k_cache)
        v_new = jnp.where(is_slot, new_value, v_cache)
        scores = jnp.einsum('bkgd,btkd->bkgt', query, k_new, preferred_element_type=jnp.float32) * head_dim ** -0.5
        valid_mask = (slot_ids[None, :] <= positions[:, None])[:, None, None, :]
        scores = jnp.where(valid_mask, scores, -jnp.inf)
        local_max = jnp.max(scores, axis=-1)
        safe_max = jnp.where(jnp.isfinite(local_max), local_max, 0.0)
        weights = jnp.exp(scores - safe_max[..., None])
        local_sum = jnp.sum(weights, axis=-1)
        local_mix = jnp.einsum('bkgt,btkd->bkgd', weights.astype(jnp.bfloat16), v_new, preferred_element_type=jnp.float32)
        global_max = lax.pmax(local_max, 'seq')
        rescale = jnp.exp(local_max - global_max)
        total_sum, total_mix = lax.psum((local_sum * rescale, local_mix * rescale[..., None]), 'seq')
        attn_flat = (total_mix / total_sum[..., None]).astype(jnp.bfloat16).reshape(batch_size, q_cols)
        attn_part = lax.dynamic_slice_in_dim(attn_flat, seq_idx * wo_rows, wo_rows, axis=1)
        y_part = jnp.dot(attn_part, w_out, preferred_element_type=jnp.float32)
        y_total = lax.psum(y_part, ('head', 'seq'))
        return y_total.astype(jnp.bfloat16), k_new, v_new

    return jax.shard_map(
        local_step,
        mesh=mesh,
        in_specs=(P('rep', None), P(), P(), P(), P(('head', 'seq'), None), cache_spec, cache_spec, P('rep')),
        out_specs=(P('rep', None), cache_spec, cache_spec),
        check_vma=False,
    )
```

profile of v0, /device:TPU:0, one launch (start us, length us, event | category | flops | bytes accessed | tf_op | source)
XLA Modules:
  0.0 190.7 jit_solution(13100304915797613230)
XLA Ops:
  7.2 0.0 copy-start
  7.2 0.0 copy-start.1
  7.2 0.0 copy-start.4
  7.2 0.0 all-reduce.3.cloned.1.call-start
  7.3 7.1 %fusion.19 = bf16[32,2048]{1,0:T(8,128)(2,1)S(1)} fusion(bf16[32,3072]{1,0:T(8,128)(2,1)} %param.8, bf16[3072,4096]{1,0:T(8,128)(2,1)} %param.9, s32[]{:T(128)S(6)} %select_n.30), kind=kOutput, calls=%fused_computation.15 | convolution fusion | flops 402718720 | bytes 12910596 | tf_op jit(solution)/shard_map/dot_general | solution.py:23
  14.4 0.9 reshape.109
  15.2 7.0 %fusion.13 = bf16[2048,32]{0,1:T(8,128)(2,1)S(1)} fusion(bf16[32,3072]{1,0:T(8,128)(2,1)} %param.8, bf16[3072,4096]{1,0:T(8,128)(2,1)} %param.10, s32[]{:T(128)S(6)} %select_n.30), kind=kOutput, calls=%fused_computation.13 | convolution fusion | flops 402718720 | bytes 12910596 | tf_op jit(solution)/shard_map/dot_general | solution.py:24
  22.2 0.0 copy-done.1
  22.2 6.8 %fusion.16 = bf16[2048,32]{0,1:T(8,128)(2,1)S(1)} fusion(bf16[32,3072]{1,0:T(8,128)(2,1)S(1)} %copy-done.1, bf16[3072,4096]{1,0:T(8,128)(2,1)} %param.11, s32[]{:T(128)S(6)} %select_n.30), kind=kOutput, calls=%fused_computation.14 | convolution fusion | flops 402718720 | bytes 12910596 | tf_op jit(solution)/shard_map/dot_general | solution.py:25
  29.1 0.0 copy-done.4
  29.1 0.1 broadcast_compare_fusion.1
  29.2 0.0 copy-start.2
  29.2 44.5 %broadcast_select_fusion.1 = (bf16[32,256,8,256]{3,2,1,0:T(8,128)(2,1)}, bf16[32,256,8,256]{3,2,1,0:T(8,128)(2,1)}) fusion(bf16[32,256,8,256]{3,2,1,0:T(8,128)(2,1)} %param.13, pred[32,256]{1,0:T(8,128)(4,1)S(1)} %get-tuple-element.10, bf16[32,8,256]{2,1,0:T(8,128)(2,1)S(1)} %bitcast.51, bf16[32,256,8,256]{3,2,1,0:T(8,128)(2,1)} %param.14, ...), kind=kLoop, calls=%fused_computation.5 | loop fusion | flops 33554432 | bytes 134488064 | tf_op jit(solution)/shard_map/jit(_where)/select_n | solution.py:28
  73.8 18.1 %fusion.2 = f32[32,8,1,256]{3,2,1,0:T(1,128)S(1)} fusion(bf16[32,8,256,1]{2,3,1,0:T(2,128)(2,1)} %reshape.109, bf16[32,256,8,256]{3,2,1,0:T(8,128)(2,1)} %get-tuple-element.7), kind=kOutput, calls=%fused_computation.2 | convolution fusion | flops 33554432 | bytes 33947648 | tf_op jit(solution)/shard_map/bkgd,btkd->bkgt/dot_general | solution.py:30
  91.9 0.0 copy-done.2
  91.9 0.1 fusion.27
  92.0 0.6 is-finite_select_fusion
  92.6 13.7 %pmax.7 = f32[32,8,1]{1,0,2:T(8,128)} all-reduce(f32[32,8,1]{1,0,2:T(8,128)S(1)} %bitcast.53), channel_id=1, replica_groups=mesh['rep'=1,'head'=2,'seq'=4] {'seq'}, use_global_device_ids=true, to_apply=%region_1.2 | all-reduce | flops 256 | bytes 2048 | tf_op jit(solution)/shard_map/pmax | solution.py:38
  106.3 0.9 fusion.25
  107.2 1.3 fusion.31
  108.5 0.0 copy-start.3
  108.5 19.0 %fusion = f32[32,8,1,256]{3,2,1,0:T(1,128)S(1)} fusion(bf16[32,256,8,256]{3,2,1,0:T(8,128)(2,1)} %get-tuple-element.8, bf16[32,8,256,1]{2,1,0,3:T(8,128)(2,1)S(1)} %get-tuple-element.4), kind=kOutput, calls=%fused_computation | convolution fusion | flops 33554432 | bytes 33947648 | tf_op jit(solution)/shard_map/bkgt,btkd->bkgd/dot_general | solution.py:37
  127.6 0.0 copy-done.3
  127.6 0.8 fusion.22
  128.4 0.0 all-reduce.3.cloned.1.call-update
  128.4 11.1 %psum.22 = f32[32,8]{1,0:T(8,128)S(1)} all-reduce(f32[32,8]{1,0:T(8,128)} %get-tuple-element.5), channel_id=1, replica_groups=mesh['rep'=1,'head'=2,'seq'=4] {'seq'}, use_global_device_ids=true, to_apply=%region_4.5 | all-reduce | flops 256 | bytes 2048 | tf_op jit(solution)/shard_map/psum | solution.py:40
  139.5 15.7 %all-reduce.3.cloned.1.call-done = f32[32,8,1,256]{3,1,0,2:T(8,128)} async-done(((f32[32,8,1,256]{3,1,0,2:T(8,128)}), f32[32,8,1,256]{3,1,0,2:T(8,128)}) %all-reduce.3.cloned.1.call-update) | async-done | bytes 262160 | tf_op jit(solution)/shard_map/psum | solution.py:40
  155.2 1.1 divide_convert_fusion
  156.3 0.0 copy-done
  156.3 0.6 fusion.29
  157.0 26.8 %all-reduce.4 = bf16[32,3072]{1,0:T(8,128)(2,1)} all-reduce(f32[32,3072]{1,0:T(8,128)S(1)} %fusion.29), channel_id=1, replica_groups=mesh['rep'=1,'head'=2,'seq'=4] {'head','seq'}, use_global_device_ids=true, to_apply=%region_5.6 | all-reduce | flops 98304 | bytes 589824 | tf_op jit(solution)/shard_map/psum | solution.py:44
  (4 shorter events, 0.1 us)
Async XLA Ops:
  7.2 149.2 %copy-start = (bf16[512,3072]{1,0:T(8,128)(2,1)S(1)}, bf16[512,3072]{1,0:T(8,128)(2,1)}, u32[]{:S(2)}) copy-start(bf16[512,3072]{1,0:T(8,128)(2,1)} %param.12) | copy-start | bytes 9437188
  7.2 15.1 %copy-start.1 = (bf16[32,3072]{1,0:T(8,128)(2,1)S(1)}, bf16[32,3072]{1,0:T(8,128)(2,1)}, u32[]{:S(2)}) copy-start(bf16[32,3072]{1,0:T(8,128)(2,1)} %param.8) | copy-start | bytes 589828
  7.2 21.9 %copy-start.4 = (s32[32]{0:T(128)S(1)}, s32[32]{0:T(128)}, u32[]{:S(2)}) copy-start(s32[32]{0:T(128)} %param.15) | copy-start | bytes 388
  7.2 148.0 %all-reduce.3.cloned.1.call-start = ((), (), s32[]{:S(2)}) async-start(), calls=%async_computation | async-start | bytes 524288 | tf_op jit(solution)/shard_map/psum | solution.py:40
  29.2 62.7 %copy-start.2 = (pred[32,256]{1,0:T(8,128)(4,1)}, pred[32,256]{1,0:T(8,128)(4,1)S(1)}, u32[]{:S(2)}) copy-start(pred[32,256]{1,0:T(8,128)(4,1)S(1)} %get-tuple-element.9) | copy-start | bytes 24580
  108.5 19.0 %copy-start.3 = (f32[32,8]{1,0:T(8,128)S(1)}, f32[32,8]{1,0:T(8,128)}, u32[]{:S(2)}) copy-start(f32[32,8]{1,0:T(8,128)} %get-tuple-element.6) | copy-start | bytes 3076
Sparse Core Ops, SparseCore 0:
  128.5 26.6 all-reduce.2
where the time goes:
time: 191 us
  matrix products  58.7 us (31%)
  blocking collectives  51.6 us (27%)
  other arithmetic  49.5 us (26%)
  waiting for transfers between devices  15.7 us (8%)
  between operations  14.2 us (7%)
    select_n x1, other arithmetic, local_step(): k_new = jnp.where(is_slot, new_key, k_cache)  44.5 us
    psum x1, blocking collectives, local_step(): y_total = lax.psum(y_part, ('head', 'seq'))  26.8 us
    dot_general x1, matrix products, local_step(): jnp.einsum('bkgt,btkd->bkgd', weights.astype(jnp.bfloat16), v_new, prefer...  19 us
    dot_general x1, matrix products, local_step(): jnp.einsum('bkgd,btkd->bkgt', query, k_new, preferred_element_type=jnp.fl...  18.1 us
    psum x1, waiting for transfers between devices, local_step(): lax.psum((local_sum * rescale, local_mix * rescale[..., None]), 'seq')  15.7 us
    pmax x1, blocking collectives, local_step(): global_max = lax.pmax(local_max, 'seq')  13.7 us
    psum x1, blocking collectives, local_step(): lax.psum((local_sum * rescale, local_mix * rescale[..., None]), 'seq')  11.1 us
    dot_general x1, matrix products, local_step(): jnp.dot(tokens, wq_local, preferred_element_type=jnp.float32)  7.09 us
  transfers between devices with their start and end apart: 1, of which 1 were waited for; matrix products, arithmetic and copies ran while one was open for 0% of the time, Pallas kernels for 0%

commit v1 on v0

v1 whole, which is shorter than its diff:
```python
import functools

import jax
import jax.numpy as jnp
from jax import lax
from jax.experimental import pallas as pl
from jax.experimental.pallas import tpu as pltpu
from jax.sharding import PartitionSpec as P

MESH = pl.DeviceIdType.MESH
RING = 12
AHEAD = 8
PARTS = 4
F32 = jnp.float32
BF16 = jnp.bfloat16
NT = (((1,), (1,)), ((), ()))


def _at(h, s):
    return {"head": h, "seq": s}


def _greet(peers):
    barrier = pltpu.get_barrier_semaphore()
    for peer in peers:
        pl.semaphore_signal(barrier, inc=1, device_id=peer, device_id_type=MESH)
    return lambda: pl.semaphore_wait(barrier, len(peers))


def project_kernel(x_ref, wq_ref, wk_ref, wv_ref, k_hbm, v_hbm,
                   qkv_ref, kring, vring,
                   wbuf, held, wsem, ringsem, ssem, rsem):
    nseq = held.shape[0]
    h, s = lax.axis_index("head"), lax.axis_index("seq")
    cols = wbuf.shape[-1]
    rows = wbuf.shape[2]
    first = pl.multiple_of((h * nseq + s) * cols, 128)
    peers = [lax.rem(s + d, nseq) for d in range(1, nseq)]
    joined = _greet([_at(h, p) for p in peers])
    loads = []
    for j, w in enumerate((wq_ref, wk_ref, wv_ref)):
        for p in range(PARTS):
            c = pltpu.make_async_copy(
                w.at[pl.ds(p * rows, rows), pl.ds(first, cols)], wbuf.at[j, p], wsem.at[j, p])
            c.start()
            loads.append(c)
    ring = []
    for b in range(AHEAD):
        for i, (src, dst) in enumerate(((k_hbm, kring), (v_hbm, vring))):
            c = pltpu.make_async_copy(src.at[b], dst.at[b], ringsem.at[i, b])
            c.start()
            ring.append(c)
    for j in range(3):
        acc = None
        for p in range(PARTS):
            loads[j * PARTS + p].wait()
            part = jnp.dot(x_ref[:, p * rows:(p + 1) * rows], wbuf[j, p], preferred_element_type=F32)
            acc = part if acc is None else acc + part
        held[s, j] = acc.astype(BF16)
    joined()
    sends = []
    for i, p in enumerate(peers):
        c = pltpu.make_async_remote_copy(
            src_ref=held.at[s], dst_ref=held.at[s], send_sem=ssem.at[i], recv_sem=rsem.at[i],
            device_id=_at(h, p), device_id_type=MESH)
        c.start()
        sends.append(c)

    def spread(src):
        per = cols // 256
        for j in range(3):
            for i in range(per):
                for half in range(2):
                    val = held[src, j, :, i * 256 + half * 128:i * 256 + half * 128 + 128].astype(F32)
                    qkv_ref[j, half, pl.ds(src * per + i, val.shape[0], stride=nseq * per), :] = val

    spread(s)
    for i in range(nseq - 1):
        sends[i].wait_recv()
        spread(lax.rem(s + nseq - 1 - i, nseq))
    for c in sends:
        c.wait_send()
    for c in ring:
        c.wait()


def attend_kernel(scale, pos_ref, qkv_ref, k_hbm, v_hbm, kring_in, vring_in,
                  ko_hbm, vo_hbm, part_ref, stat_ref, kring, vring,
                  obuf, mbuf, lbuf, kin, vin, kout, vout):
    batch, wide, hd = k_hbm.shape
    heads = part_ref.shape[0]
    span = wide // heads
    base = lax.axis_index("seq") * span
    col = lax.broadcasted_iota(jnp.int32, (heads, wide), 1)
    row = lax.broadcasted_iota(jnp.int32, (heads, wide), 0)
    own = lax.rem(col, heads) == row
    slot_of = base + col // heads

    def fresh(j, lines):
        return jnp.concatenate([qkv_ref[j, 0, lines, :], qkv_ref[j, 1, lines, :]], axis=-1).astype(BF16)

    def body(b, carry):
        slot = lax.rem(b, RING)
        nxt = b + AHEAD

        @pl.when(nxt < batch)
        def _():
            ns = lax.rem(nxt, RING)

            @pl.when(nxt >= RING)
            def _():
                pltpu.make_async_copy(kring.at[ns], ko_hbm.at[nxt - RING], kout.at[ns]).wait()
                pltpu.make_async_copy(vring.at[ns], vo_hbm.at[nxt - RING], vout.at[ns]).wait()

            pltpu.make_async_copy(k_hbm.at[nxt], kring.at[ns], kin.at[ns]).start()
            pltpu.make_async_copy(v_hbm.at[nxt], vring.at[ns], vin.at[ns]).start()

        pos = pos_ref[b]
        at = pos - base
        mine = jnp.logical_and(at >= 0, at < span)
        lines = pl.ds(pl.multiple_of(b * heads, heads), heads)
        spot = pl.ds(pl.multiple_of(at * heads, heads), heads)

        @pl.when(b >= AHEAD)
        def _():
            pltpu.make_async_copy(k_hbm.at[b], kring.at[slot], kin.at[slot]).wait()

        @pl.when(mine)
        def _():
            kring[slot, spot, :] = fresh(1, lines)

        query = fresh(0, lines)
        keys = kring[slot]
        score = lax.dot_general(query, keys, NT, preferred_element_type=F32) * scale
        pltpu.make_async_copy(kring.at[slot], ko_hbm.at[b], kout.at[slot]).start()
        score = jnp.where(jnp.logical_and(own, slot_of <= pos), score, -jnp.inf)
        top = jnp.max(score, axis=-1, keepdims=True)
        safe = jnp.where(top == -jnp.inf, 0.0, top)
        weight = jnp.exp(score - safe)
        total = jnp.sum(weight, axis=-1, keepdims=True)

        @pl.when(b >= AHEAD)
        def _():
            pltpu.make_async_copy(v_hbm.at[b], vring.at[slot], vin.at[slot]).wait()

        @pl.when(mine)
        def _():
            vring[slot, spot, :] = fresh(2, lines)

        values = vring[slot]
        mix = jnp.dot(weight.astype(BF16), values, preferred_element_type=F32)
        obuf[0, lines, :] = mix[:, :128]
        obuf[1, lines, :] = mix[:, 128:]
        pltpu.make_async_copy(vring.at[slot], vo_hbm.at[b], vout.at[slot]).start()
        mbuf[lines, :] = jnp.broadcast_to(top, (heads, 128))
        lbuf[lines, :] = jnp.broadcast_to(total, (heads, 128))
        return carry

    lax.fori_loop(0, batch, body, 0)
    eye = (lax.broadcasted_iota(jnp.int32, (batch, 128), 0)
           == lax.broadcasted_iota(jnp.int32, (batch, 128), 1))
    for hh in range(heads):
        pick = pl.ds(hh, batch, stride=heads)
        part_ref[hh, :, :128] = obuf[0, pick, :]
        part_ref[hh, :, 128:] = obuf[1, pick, :]
        stat_ref[hh, 0:1, :] = jnp.sum(jnp.where(eye, mbuf[pick, :], 0.0), axis=0, keepdims=True)
        stat_ref[hh, 1:2, :] = jnp.sum(jnp.where(eye, lbuf[pick, :], 0.0), axis=0, keepdims=True)
    def drain(i, carry):
        b = batch - RING + i
        ns = lax.rem(b, RING)
        pltpu.make_async_copy(kring.at[ns], ko_hbm.at[b], kout.at[ns]).wait()
        pltpu.make_async_copy(vring.at[ns], vo_hbm.at[b], vout.at[ns]).wait()
        return carry

    lax.fori_loop(0, RING, drain, 0)


def finish_kernel(part_ref, stat_ref, wo_hbm, y_ref,
                  gpart, gstat, wo, ysend, ygot, yout,
                  wsem, s1, r1, s2, r2, s3, r3, s4, r4):
    nseq = gpart.shape[0]
    per, batch, hd = gpart.shape[1:]
    ndev = ysend.shape[0]
    cols = ysend.shape[-1]
    h, s = lax.axis_index("head"), lax.axis_index("seq")
    me = h * nseq + s
    far = [lax.rem(me + d, ndev) for d in range(1, ndev)]
    joined = _greet([_at(p // nseq, lax.rem(p, nseq)) for p in far])
    load = pltpu.make_async_copy(wo_hbm, wo, wsem)
    load.start()
    joined()
    near = [lax.rem(s + d, nseq) for d in range(1, nseq)]
    sends = []
    for i, p in enumerate(near):
        c = pltpu.make_async_remote_copy(
            src_ref=part_ref.at[pl.ds(p * per, per)], dst_ref=gpart.at[i], send_sem=s1.at[i],
            recv_sem=r1.at[i], device_id=_at(h, p), device_id_type=MESH)
        d = pltpu.make_async_remote_copy(
            src_ref=stat_ref.at[pl.ds(p * per, per)], dst_ref=gstat.at[i], send_sem=s4.at[i],
            recv_sem=r4.at[i], device_id=_at(h, p), device_id_type=MESH)
        c.start()
        d.start()
        sends += [c, d]
    for c in sends:
        c.wait_recv()
    eye = (lax.broadcasted_iota(jnp.int32, (batch, 128), 0)
           == lax.broadcasted_iota(jnp.int32, (batch, 128), 1))
    y = None
    load.wait()
    for e in range(per):
        mine = stat_ref[s * per + e]
        stats = [mine] + [gstat[i, e] for i in range(nseq - 1)]
        parts = [part_ref[s * per + e]] + [gpart[i, e] for i in range(nseq - 1)]
        top = functools.reduce(jnp.maximum, [t[0:1] for t in stats])
        mix, total = None, None
        for t, part in zip(stats, parts):
            factor = jnp.exp(t[0:1] - top)
            line = factor * t[1:2]
            total = line if total is None else total + line
            down = jnp.sum(jnp.where(eye, factor, 0.0), axis=1, keepdims=True)
            mix = part * down if mix is None else mix + part * down
        down = jnp.sum(jnp.where(eye, total, 0.0), axis=1, keepdims=True)
        attn = (mix / down).astype(BF16)
        term = jnp.dot(attn, wo[e * hd:(e + 1) * hd, :], preferred_element_type=F32)
        y = term if y is None else y + term
    for p in range(ndev):
        ysend[p] = y[:, p * cols:(p + 1) * cols]
    moves = []
    for i, p in enumerate(far):
        c = pltpu.make_async_remote_copy(
            src_ref=ysend.at[p], dst_ref=ygot.at[i], send_sem=s2.at[i], recv_sem=r2.at[i],
            device_id=_at(p // nseq, lax.rem(p, nseq)), device_id_type=MESH)
        c.start()
        moves.append(c)
    acc = ysend[me]
    for i, c in enumerate(moves):
        c.wait_recv()
        acc = acc + ygot[i]
    yout[me] = acc.astype(BF16)
    shares = []
    for i, p in enumerate(far):
        c = pltpu.make_async_remote_copy(
            src_ref=yout.at[me], dst_ref=yout.at[me], send_sem=s3.at[i], recv_sem=r3.at[i],
            device_id=_at(p // nseq, lax.rem(p, nseq)), device_id_type=MESH)
        c.start()
        shares.append(c)
    for c in shares:
        c.wait_recv()
    for p in range(ndev):
        y_ref[:, p * cols:(p + 1) * cols] = yout[p]
    for c in sends + moves + shares:
        c.wait_send()


def solution(mesh):
    nhead, nseq = mesh.shape["head"], mesh.shape["seq"]
    ndev = nhead * nseq
    cache_spec = P("rep", "seq", "head", None)
    any_spec = pl.BlockSpec(memory_space=pl.ANY)
    vmem = pl.BlockSpec(memory_space=pltpu.VMEM)
    smem = pl.BlockSpec(memory_space=pltpu.SMEM)

    def local_step(tokens, w_query, w_key, w_value, w_out, k_cache, v_cache, positions):
        batch, span, heads, hd = k_cache.shape
        model = tokens.shape[1]
        cols = heads * hd // nseq
        per = heads // nseq
        ring = jax.ShapeDtypeStruct((RING, span * heads, hd), BF16)
        cache = jax.ShapeDtypeStruct((batch, span * heads, hd), BF16)
        k_flat, v_flat = k_cache.reshape(cache.shape), v_cache.reshape(cache.shape)
        dma = pltpu.SemaphoreType.DMA
        qkv, kring, vring = pl.pallas_call(
            project_kernel,
            out_shape=(jax.ShapeDtypeStruct((3, 2, batch * heads, 128), F32), ring, ring),
            in_specs=[vmem] + [any_spec] * 5,
            out_specs=(vmem, vmem, vmem),
            scratch_shapes=[
                pltpu.VMEM((3, PARTS, model // PARTS, cols), BF16),
                pltpu.VMEM((nseq, 3, batch, cols), BF16),
                dma((3, PARTS)), dma((2, AHEAD)), dma((nseq - 1,)), dma((nseq - 1,)),
            ],
            compiler_params=pltpu.CompilerParams(
                collective_id=0, has_side_effects=True, vmem_limit_bytes=14 * 2**20),
        )(tokens, w_query, w_key, w_value, k_flat, v_flat)
        k_out, v_out, part, stat, _, _ = pl.pallas_call(
            functools.partial(attend_kernel, hd ** -0.5),
            out_shape=(cache, cache, jax.ShapeDtypeStruct((heads, batch, hd), F32),
                       jax.ShapeDtypeStruct((heads, 8, 128), F32), ring, ring),
            in_specs=[smem, vmem, any_spec, any_spec, vmem, vmem],
            out_specs=(any_spec, any_spec, vmem, vmem, vmem, vmem),
            input_output_aliases={4: 4, 5: 5},
            scratch_shapes=[
                pltpu.VMEM((2, batch * heads, 128), F32),
                pltpu.VMEM((batch * heads, 128), F32),
                pltpu.VMEM((batch * heads, 128), F32),
                dma((RING,)), dma((RING,)), dma((RING,)), dma((RING,)),
            ],
            compiler_params=pltpu.CompilerParams(vmem_limit_bytes=8 * 2**20),
        )(positions, qkv, k_flat, v_flat, kring, vring)
        ycols = model // ndev
        y = pl.pallas_call(
            finish_kernel,
            out_shape=jax.ShapeDtypeStruct((batch, model), BF16),
            in_specs=[vmem, vmem, any_spec],
            out_specs=vmem,
            scratch_shapes=[
                pltpu.VMEM((nseq, per, batch, hd), F32),
                pltpu.VMEM((nseq, per, 8, 128), F32),
                pltpu.VMEM(w_out.shape, BF16),
                pltpu.VMEM((ndev, batch, ycols), F32),
                pltpu.VMEM((ndev, batch, ycols), F32),
                pltpu.VMEM((ndev, batch, ycols), BF16),
                dma, dma((nseq,)), dma((nseq,)), dma((ndev,)), dma((ndev,)),
                dma((ndev,)), dma((ndev,)), dma((nseq,)), dma((nseq,)),
            ],
            compiler_params=pltpu.CompilerParams(
                collective_id=1, has_side_effects=True, vmem_limit_bytes=12 * 2**20),
        )(part, stat, w_out)
        return y, k_out.reshape(k_cache.shape), v_out.reshape(v_cache.shape)

    return jax.shard_map(
        local_step,
        mesh=mesh,
        in_specs=(P("rep", None), P(), P(), P(), P(("head", "seq"), None), cache_spec, cache_spec, P("rep")),
        out_specs=(P("rep", None), cache_spec, cache_spec),
        check_vma=False,
    )
```

time: 191 us -> 75.6 us (0.40)
  Pallas kernels: 0 us -> 73.2 us
  matrix products: 58.7 us -> 0 us
  blocking collectives: 51.6 us -> 0 us
  other arithmetic: 49.5 us -> 0 us
  waiting for transfers between devices: 15.7 us -> 0 us
  between operations: 14.2 us -> 0.69 us
    pallas_call x0 -> x3, Pallas kernels: none -> 73.2 us  [the longest x1 39.2 us: local_step(): pl.pallas_call(functools.partial(attend_kernel, hd ** (-0.5)), out_shape=...]
    dot_general x6 -> x0, matrix products: 58.7 us -> none  [the longest x1 19 us: local_step(): jnp.einsum('bkgt,btkd->bkgd', weights.astype(jnp.bfloat16), v_new, prefer...]
    select_n x2 -> x0, other arithmetic: 45.1 us -> none  [the longest x1 44.5 us: local_step(): k_new = jnp.where(is_slot, new_key, k_cache)]
    psum x2 -> x0, blocking collectives: 38 us -> none  [the longest x1 26.8 us: local_step(): y_total = lax.psum(y_part, ('head', 'seq'))]
    psum x1 -> x0, waiting for transfers between devices: 15.7 us -> none  [local_step(): lax.psum((local_sum * rescale, local_mix * rescale[..., None]), 'seq')]
    pmax x1 -> x0, blocking collectives: 13.7 us -> none  [local_step(): global_max = lax.pmax(local_max, 'seq')]
  transfers between devices with their start and end apart: 1 -> 0, of which waited for: 1 -> 0; matrix products, arithmetic and copies ran while one was open for 0% -> 0% of each run, Pallas kernels for 0% -> 0%
where the time goes in v1:
time: 75.6 us; the launch traced here: 75.5 us
  Pallas kernels  73.2 us (97%)
  local copies, waits for them, and re-layouts  1.61 us (2%)
    pallas_call x1, Pallas kernels, local_step(): pl.pallas_call(functools.partial(attend_kernel, hd ** (-0.5)), out_shape=...  39.2 us
    pallas_call x1, Pallas kernels, local_step(): pl.pallas_call(finish_kernel, out_shape=jax.ShapeDtypeStruct((batch, mode...  18.2 us
    pallas_call x1, Pallas kernels, local_step(): pl.pallas_call(project_kernel, out_shape=(jax.ShapeDtypeStruct((3, 2, bat...  15.9 us
    unnamed x7, local copies, waits for them, and re-layouts  1.61 us

profile of v1, /device:TPU:0, one launch (start us, length us, event | category | flops | bytes accessed | tf_op | source)
XLA Modules:
  0.0 75.5 jit_solution(1838117880268216144)
XLA Ops:
  0.6 0.0 copy-start.1
  0.6 0.9 %copy-done.1 = bf16[32,3072]{1,0:T(8,128)(2,1)S(1)} copy-done((bf16[32,3072]{1,0:T(8,128)(2,1)S(1)}, bf16[32,3072]{1,0:T(8,128)(2,1)}, u32[]{:S(2)}) %copy-start.1) | copy-done | bytes 196632
  1.6 0.0 copy-start.2
  1.6 15.9 %shard_map.103 = (f32[3,2,256,128]{3,2,1,0:T(8,128)S(1)}, bf16[12,2048,256]{2,1,0:T(8,128)(2,1)S(1)}, bf16[12,2048,256]{2,1,0:T(8,128)(2,1)S(1)}) custom-call(bf16[32,3072]{1,0:T(8,128)(2,1)S(1)} %copy-done.1, bf16[3072,4096]{1,0:T(8,128)(2,1)} %wq_ref.1, bf16[3072,4096]{1,0:T(8,128)(2,1)} %wk_ref.1, bf16[3072,4096]{1,0:T(8,128)(2,1)} %wv_ref.1, ...), custom_call_target="tpu_custom_call" | custom-call | tf_op jit(solution)/shard_map/pallas_call | solution.py:272
  17.4 0.0 copy-done.2
  17.4 0.0 copy-start
  17.4 39.2 %shard_map.104 = (bf16[32,2048,256]{2,1,0:T(8,128)(2,1)}, bf16[32,2048,256]{2,1,0:T(8,128)(2,1)}, f32[8,32,256]{2,1,0:T(8,128)S(1)}, f32[8,8,128]{2,1,0:T(8,128)...) custom-call(s32[32]{0:T(128)S(1)} %copy-done.2, ...), custom_call_target="tpu_custom_call", output_to_operand_aliasing={{4}: (4, {}), {5}: (5, {})} | custom-call | tf_op jit(solution)/shard_map/pallas_call | solution.py:285
  56.6 0.0 copy-done
  56.7 18.2 %shard_map.105 = bf16[32,3072]{1,0:T(8,128)(2,1)S(1)} custom-call(f32[8,32,256]{2,1,0:T(8,128)S(1)} %get-tuple-element.13.part_ref, f32[8,8,128]{2,1,0:T(8,128)S(1)} %get-tuple-element.14.stat_ref, bf16[512,3072]{1,0:T(8,128)(2,1)S(1)} %copy-done), custom_call_target="tpu_custom_call" | custom-call | tf_op jit(solution)/shard_map/pallas_call | solution.py:301
  74.8 0.7 copy.16
Async XLA Ops:
  0.6 0.9 %copy-start.1 = (bf16[32,3072]{1,0:T(8,128)(2,1)S(1)}, bf16[32,3072]{1,0:T(8,128)(2,1)}, u32[]{:S(2)}) copy-start(bf16[32,3072]{1,0:T(8,128)(2,1)} %x_ref.1) | copy-start | bytes 589828
  1.6 15.9 %copy-start.2 = (s32[32]{0:T(128)S(1)}, s32[32]{0:T(128)}, u32[]{:S(2)}) copy-start(s32[32]{0:T(128)} %pos_ref.1) | copy-start | bytes 388
  17.4 39.2 %copy-start = (bf16[512,3072]{1,0:T(8,128)(2,1)S(1)}, bf16[512,3072]{1,0:T(8,128)(2,1)}, u32[]{:S(2)}) copy-start(bf16[512,3072]{1,0:T(8,128)(2,1)} %wo_hbm.1) | copy-start | bytes 9437188
